TPU v7x, 32 devices: a whole 2x2x4 slice. The times are simulated.
32 devices in a mesh: ta: 16 (over z, x, core), aa: 2 (over y).
Axes of the slice: x: 2, y: 2, z: 4, core: 2. Of those that a mesh axis runs over, the one named last changes fastest.
Arguments:
- voltages: bfloat16 [256, 393216], P('aa', 'ta'), may hold values from -6 to 6
- pfb_window: float32 [4, 8192], replicated, may hold values from -3 to 3
Outputs:
- visibilities: float32 [2048, 256, 512], P('ta', 'aa')
All inputs are finite; a program needn't handle non-finite values.
Results may differ from a plain program's by a relative error of at most 0.0026.
Values may be sent and summed in bfloat16 or wider, within the bound.
A program may use at most 192 MiB of HBM per device.

v0:
```python
import math
import jax
import jax.numpy as jnp
from jax import lax
from jax.sharding import PartitionSpec as P

NFFT = 8192
CH = 2048
TAPS = 4
CH_OFF = 1024


def shifted(x, axis, by):
    peers = lax.axis_size(axis)
    pairs = [(i, i + by) for i in range(peers) if 0 <= i + by < peers]
    return lax.ppermute(x, axis, pairs)


def tables(row_count, col_count, modulus, offset):
    row_index = lax.broadcasted_iota(jnp.int32, (row_count, col_count), 0)
    col_index = lax.broadcasted_iota(jnp.int32, (row_count, col_count), 1) + offset
    phases = row_index * col_index % modulus
    angles = phases.astype(jnp.float32) * (2.0 * math.pi / modulus)
    return (jnp.cos(angles), jnp.sin(angles))


def with_quadrature(spectra):
    swapped = jnp.stack([spectra[:, :, 1], -spectra[:, :, 0]], axis=2)
    return jnp.concatenate([spectra, swapped], axis=3)


def products(left_rows, right_cols):
    return jnp.einsum("cfpi,cfpj->cij", left_rows, right_cols, preferred_element_type=jnp.float32)


def channelize(filtered):
    signal_count = filtered.shape[0]
    frame_count = filtered.shape[1]
    section_one = 64
    section_two = NFFT // section_one
    highest = lax.Precision.HIGHEST
    blocks = filtered.reshape(signal_count, frame_count, section_one, section_two)
    cosine_one, sine_one = tables(section_one, section_one, section_one, 0)
    section_real = jnp.einsum("sfan,ak->sfkn", blocks, cosine_one, precision=highest)
    section_imag = -jnp.einsum("sfan,ak->sfkn", blocks, sine_one, precision=highest)
    cosine_twist, sine_twist = tables(section_one, section_two, NFFT, 0)
    twist_real = section_real * cosine_twist + section_imag * sine_twist
    twist_imag = section_imag * cosine_twist - section_real * sine_twist
    cosine_two, sine_two = tables(
        section_two, CH // section_one, section_two, CH_OFF // section_one
    )
    scaling = 1.0 / math.sqrt(NFFT)
    spec_real = (
        jnp.einsum("sfkn,nm->mkfs", twist_real, cosine_two, precision=highest)
        + jnp.einsum("sfkn,nm->mkfs", twist_imag, sine_two, precision=highest)
    ) * scaling
    spec_imag = (
        jnp.einsum("sfkn,nm->mkfs", twist_imag, cosine_two, precision=highest)
        - jnp.einsum("sfkn,nm->mkfs", twist_real, sine_two, precision=highest)
    ) * scaling
    return jnp.stack([spec_real, spec_imag], axis=3).reshape(CH, frame_count, 2, signal_count)


def filter_frames(extended, pfb_window, frame_count):
    filtered = jnp.zeros((extended.shape[0], frame_count, NFFT), jnp.float32)
    for tap_index in range(TAPS):
        filtered = filtered + pfb_window[tap_index] * extended[
            :, tap_index : tap_index + frame_count, :
        ].astype(jnp.float32)
    return filtered


def per_device(voltages, pfb_window):
    signal_count = voltages.shape[0]
    frame_count = voltages.shape[1] // NFFT
    history = shifted(voltages, "ta", 1)
    extended = jnp.concatenate([history, voltages], axis=1).reshape(
        signal_count, frame_count + TAPS - 1, NFFT
    )
    filtered = filter_frames(extended, pfb_window, frame_count)
    spectra = channelize(filtered).astype(jnp.bfloat16)
    owned = lax.all_to_all(spectra, "ta", split_axis=0, concat_axis=1, tiled=True)
    frames_all = owned.shape[1]
    norm_scale = 1.0 / math.sqrt(frames_all)
    left_rows = with_quadrature(owned)
    result = products(left_rows, lax.all_gather(owned, "aa", axis=3, tiled=True)) * norm_scale
    return jnp.concatenate([result[:, :signal_count], result[:, signal_count:]], axis=2)


def solution(mesh):
    in_specs = (P("aa", "ta"), P())
    out_specs = P("ta", "aa", None)
    return jax.shard_map(
        per_device, mesh=mesh, in_specs=in_specs, out_specs=out_specs, check_vma=False
    )
```

profile of v0, /device:TPU:0, one launch (start us, length us, event | category | flops | bytes accessed | tf_op | source)
XLA Modules:
  0.0 537.9 jit_solution(2451833652315403954)
XLA Ops:
  6.5 8.6 %copy.43 = bf16[128,24576]{0,1:T(8,128)(2,1)} copy(bf16[128,24576]{1,0:T(8,128)(2,1)} %param.2) | data formatting | bytes 12582912 | tf_op args[0]
  15.2 2.8 collective-permute-start
  18.0 0.1 fusion.48
  18.1 0.1 fusion.88
  18.2 9.3 %collective-permute-done = bf16[128,24576]{0,1:T(8,128)(2,1)S(1)} collective-permute-done((bf16[128,24576]{0,1:T(8,128)(2,1)}, bf16[128,24576]{0,1:T(8,128)(2,1)S(1)}, u32[]{:S(2)}, u32[]{:S(2)}) %collective-permute-start) | collective-permute-done | bytes 6291488 | tf_op jit(solution)/shard_map/ppermute | solution.py:16
  27.5 24.4 %pad_maximum_fusion.1 = bf16[128,49152]{0,1:T(8,128)(2,1)S(1)} fusion(bf16[128,24576]{0,1:T(8,128)(2,1)} %copy.43, bf16[128,24576]{0,1:T(8,128)(2,1)S(1)} %collective-permute-done), kind=kLoop, calls=%fused_computation.2 | loop fusion | flops 25165824 | bytes 25165824 | tf_op jit(solution)/shard_map/concatenate | solution.py:77
  52.0 8.4 %multiply_add_fusion = f32[128,3,8192]{0,2,1:T(8,128)} fusion(bf16[128,6,8192]{0,2,1:T(8,128)(2,1)S(1)} %bitcast.52, f32[8192]{0:T(1024)S(1)} %bitcast.62, f32[8192]{0:T(1024)S(1)} %bitcast.63, f32[8192]{0:T(1024)S(1)} %bitcast.61, f32[8192]{0:T(1024)S(1)} %bitcast.60), kind=kLoop, calls=%fused_computation.5 | loop fusion | flops 34603008 | bytes 37879808 | tf_op jit(solution)/shard_map/add | solution.py:67
  60.4 12.8 %copy.45 = f32[128,3,64,128]{3,2,1,0:T(8,128)} copy(f32[128,3,64,128]{0,3,2,1:T(8,128)} %bitcast.55) | data formatting | bytes 25165824 | tf_op jit(solution)/shard_map/reshape | solution.py:42
  73.2 16.9 %fusion.29 = f32[64,128,3,128]{3,0,2,1:T(8,128)} fusion(f32[128,3,64,128]{3,2,1,0:T(8,128)} %copy.45), kind=kOutput, calls=%fused_computation.37 | convolution fusion | flops 2415976448 | bytes 25165824 | tf_op jit(solution)/shard_map/sfan,ak->sfkn/dot_general | solution.py:45
  90.1 23.8 %add_bitcast_fusion = (f32[128,3,64,128]{3,2,1,0:T(8,128)}, f32[128,3,64,128]{3,2,1,0:T(8,128)}) fusion(f32[64,128,3,128]{3,0,2,1:T(8,128)} %fusion.29, f32[64,128]{1,0:T(8,128)S(1)} %get-tuple-element.15, f32[64,128]{1,0:T(8,128)S(1)} %get-tuple-element.16, f32[128,3,64,128]{3,2,1,0:T(8,128)} %copy.45), kind=kOutput, calls=%fused_computation.4 | convolution fusion | flops 2437996544 | bytes 50397184 | tf_op jit(solution)/shard_map/sfan,ak->sfkn/dot_general | solution.py:44
  113.9 22.7 %fusion = f32[32,128,3,64]{1,0,3,2:T(8,128)S(1)} fusion(f32[128,3,64,128]{3,2,1,0:T(8,128)} %get-tuple-element.8, s32[32]{0:T(128)S(1)} %iota_add_fusion), kind=kOutput, calls=%fused_computation.6 | convolution fusion | flops 1208016896 | bytes 15728768 | tf_op jit(solution)/shard_map/sfkn,nm->mkfs/dot_general | solution.py:58
  136.6 0.0 copy-done
  136.6 0.0 slice-start.2
  136.6 18.4 %fusion.2 = f32[32,128,3,64]{1,0,3,2:T(8,128)S(1)} fusion(f32[128,3,64,128]{3,2,1,0:T(8,128)S(1)} %copy-done, s32[32]{0:T(128)S(1)} %iota_add_fusion), kind=kOutput, calls=%fused_computation.8 | convolution fusion | flops 1208016896 | bytes 15728768 | tf_op jit(solution)/shard_map/sfkn,nm->mkfs/dot_general | solution.py:55
  155.1 0.0 slice-done
  155.1 18.3 %fusion.17 = bf16[32,64,3,128]{3,0,1,2:T(8,128)(2,1)S(1)} fusion(f32[32,128,3,64]{1,0,3,2:T(8,128)S(1)} %fusion.2, f32[128,3,64,128]{3,2,1,0:T(8,128)S(1)} %bitcast.54, s32[32]{0:T(128)S(1)} %iota_add_fusion), kind=kOutput, calls=%fused_computation.23 | convolution fusion | flops 1210376192 | bytes 17301632 | tf_op jit(solution)/shard_map/sfkn,nm->mkfs/dot_general | solution.py:54
  173.5 18.7 %fusion.20 = bf16[32,64,3,128]{3,0,1,2:T(8,128)(2,1)S(1)} fusion(f32[32,128,3,64]{1,0,3,2:T(8,128)S(1)} %fusion, f32[128,3,64,128]{3,2,1,0:T(8,128)S(1)} %bitcast.54, s32[32]{0:T(128)S(1)} %iota_add_fusion), kind=kOutput, calls=%fused_computation.24 | convolution fusion | flops 1210376192 | bytes 17301632 | tf_op jit(solution)/shard_map/sfkn,nm->mkfs/dot_general | solution.py:59
  192.2 0.6 copy.52
  192.8 0.6 copy.49
  193.4 0.3 pad_maximum_fusion.2
  193.7 28.6 %copy.53 = bf16[2048,3,2,128]{3,2,1,0:T(2,128)(2,1)S(1)} copy(bf16[2048,3,2,128]{3,0,1,2:T(8,128)(2,1)S(1)} %pad_maximum_fusion.2) | data formatting | bytes 6291456 | tf_op jit(solution)/shard_map/stack | solution.py:61
  222.3 136.9 %all_to_all.18 = bf16[2048,3,2,128]{3,2,1,0:T(2,128)(2,1)S(1)} all-to-all(bf16[2048,3,2,128]{3,2,1,0:T(2,128)(2,1)S(1)} %copy.53), channel_id=1, replica_groups=mesh['ta'=16,'aa'=2] {'ta'}, dimensions={0} | all-to-all | bytes 6291456 | tf_op jit(solution)/shard_map/all_to_all | solution.py:82
  359.2 0.4 copy.54
  359.6 0.4 copy.55
  360.0 3.7 copy.58
  363.8 0.0 all-gather.2.cloned.1.call-update
  363.8 2.2 fusion.87
  366.0 78.9 %all-gather.2.cloned.1.call-done = bf16[128,48,2,256]{3,1,2,0:T(8,128)(2,1)} async-done(((bf16[128,48,2,128]{3,1,2,0:T(8,128)(2,1)}), bf16[128,48,2,256]{3,1,2,0:T(8,128)(2,1)}) %all-gather.2.cloned.1.call-update) | async-done | bytes 6291472 | tf_op jit(solution)/shard_map/all_gather | solution.py:86
  444.9 16.4 %bitcast_multiply_fusion = f32[128,256,256]{1,2,0:T(8,128)} fusion(bf16[128,48,2,256]{3,1,2,0:T(8,128)(2,1)} %all-gather.2.cloned.1.call-done, bf16[128,48,1,128]{3,1,2,0:T(8,128)(2,1)S(1)} %get-tuple-element.10, bf16[128,48,1,128]{3,1,2,0:T(8,128)(2,1)S(1)} %get-tuple-element.9, bf16[128,48,2,128]{3,1,2,0:T(8,128)(2,1)} %copy.58), kind=kOutput, calls=%fused_computation.1 | convolution fusion | flops 1637875712 | bytes 46137344 | tf_op jit(solution)/shard_map/cfpi,cfpj->cij/dot_general | solution.py:33
  461.3 17.7 %fusion.86 = (f32[128,128,256]{1,2,0:T(8,128)S(1)}, f32[128,128,256]{1,2,0:T(8,128)}) fusion(f32[128,256,256]{1,2,0:T(8,128)} %bitcast_multiply_fusion), kind=kLoop, calls=%fused_computation.92 | loop fusion | bytes 67108864 | tf_op jit(solution)/shard_map/slice | solution.py:87
  479.0 18.3 %pad_maximum_fusion = f32[128,128,512]{1,2,0:T(8,128)} fusion(f32[128,128,256]{1,2,0:T(8,128)} %get-tuple-element.6, f32[128,128,256]{1,2,0:T(8,128)S(1)} %get-tuple-element.5), kind=kLoop, calls=%fused_computation | loop fusion | flops 8388608 | bytes 67108864 | tf_op jit(solution)/shard_map/concatenate | solution.py:87
  497.4 33.4 %copy.60 = f32[128,128,512]{2,1,0:T(8,128)} copy(f32[128,128,512]{1,2,0:T(8,128)} %pad_maximum_fusion) | data formatting | bytes 67108864 | tf_op jit(solution)/shard_map/concatenate | solution.py:87
  (10 shorter events, 0.0 us)
Async XLA Ops:
  6.5 11.6 %copy-start.1 = (f32[4,8192]{1,0:T(4,128)S(1)}, f32[4,8192]{1,0:T(4,128)}, u32[]{:S(2)}) copy-start(f32[4,8192]{1,0:T(4,128)} %param.3) | copy-start | bytes 393220
  6.5 438.3 %all-gather.2.cloned.1.call-start = ((), (), s32[]{:S(2)}) async-start(), calls=%async_computation.1 | async-start | bytes 9437184 | tf_op jit(solution)/shard_map/all_gather | solution.py:86
  15.2 12.4 %collective-permute-start = (bf16[128,24576]{0,1:T(8,128)(2,1)}, bf16[128,24576]{0,1:T(8,128)(2,1)S(1)}, u32[]{:S(2)}, u32[]{:S(2)}) collective-permute-start(bf16[128,24576]{0,1:T(8,128)(2,1)} %copy.43), channel_id=1, source_target_pairs={{0,2},{2,4},{4,6},{6,8},{8,10},{10,12},{12,14},{14,16},{16,18},{18... | collective-permute-start | bytes 18874376 | tf_op jit(solution)/shard_map/ppermute | solution.py:16
  113.8 22.8 %copy-start = (f32[128,3,64,128]{3,2,1,0:T(8,128)S(1)}, f32[128,3,64,128]{3,2,1,0:T(8,128)}, u32[]{:S(2)}) copy-start(f32[128,3,64,128]{3,2,1,0:T(8,128)} %get-tuple-element.8) | copy-start | bytes 37748740
  113.9 41.2 %slice-start = ((s8[12582912]{0:T(1024)(128)(4,1)}), s8[4194304]{0:T(1024)(128)(4,1)S(1)}, s32[]{:S(2)}) async-start(s8[12582912]{0:T(1024)(128)(4,1)} %bitcast.53), calls=%async_computation.2 | async-start | bytes 8388608
  113.9 41.2 %slice-start.1 = ((s8[12582912]{0:T(1024)(128)(4,1)}), s8[4194304]{0:T(1024)(128)(4,1)S(1)}, s32[]{:S(2)}) async-start(s8[12582912]{0:T(1024)(128)(4,1)} %bitcast.53), calls=%async_computation.3 | async-start | bytes 8388608
  136.6 18.5 %slice-start.2 = ((s8[12582912]{0:T(1024)(128)(4,1)}), s8[4194304]{0:T(1024)(128)(4,1)S(1)}, s32[]{:S(2)}) async-start(s8[12582912]{0:T(1024)(128)(4,1)} %bitcast.53), calls=%async_computation.4 | async-start | bytes 8388608
Sparse Core Ops, SparseCore 0:
  363.9 80.9 all-gather.1
where the time goes:
time: 548 us; the launch traced here: 538 us
  blocking collectives  137 us (25%)
  matrix products  135 us (25%)
  local copies, waits for them, and re-layouts  107 us (20%)
  waiting for transfers between devices  88.2 us (16%)
  other arithmetic  53.9 us (10%)
  between operations  13.8 us (3%)
    all_to_all x1, blocking collectives, per_device(): lax.all_to_all(spectra, 'ta', split_axis=0, concat_axis=1, tiled=True)  137 us
    all_gather x1, waiting for transfers between devices, per_device(): lax.all_gather(owned, 'aa', axis=3, tiled=True)  78.9 us
    concatenate x1, local copies, waits for them, and re-layouts, per_device(): jnp.concatenate([result[:, :signal_count], result[:, signal_count:]], axi...  33.4 us
    another operation x1, local copies, waits for them, and re-layouts, channelize(): jnp.stack([spec_real, spec_imag], axis=3)  28.6 us
    concatenate x1, other arithmetic, per_device(): jnp.concatenate([history, voltages], axis=1)  24.4 us
    dot_general x1, matrix products, channelize(): jnp.einsum('sfan,ak->sfkn', blocks, cosine_one, precision=highest)  23.8 us
    dot_general x1, matrix products, channelize(): jnp.einsum('sfkn,nm->mkfs', twist_imag, cosine_two, precision=highest)  22.7 us
    dot_general x1, matrix products, channelize(): jnp.einsum('sfkn,nm->mkfs', twist_real, sine_two, precision=highest)  18.7 us
  transfers between devices with their start and end apart: 2, of which 2 were waited for; matrix products, arithmetic and copies ran while one was open for 0% of the time, Pallas kernels for 0%

commit v1 on v0

--- a/solution.py
+++ b/solution.py
@@ -79,7 +79,15 @@
     )
     filtered = filter_frames(extended, pfb_window, frame_count)
     spectra = channelize(filtered).astype(jnp.bfloat16)
-    owned = lax.all_to_all(spectra, "ta", split_axis=0, concat_axis=1, tiled=True)
+    owned = jnp.concatenate(
+        lax.all_to_all(
+            jnp.stack(jnp.split(spectra, lax.psum(1, axis_name="ta"), axis=0), axis=0),
+            split_axis=0,
+            concat_axis=0,
+            axis_name="ta",
+        ),
+        axis=1,
+    )
     frames_all = owned.shape[1]
     norm_scale = 1.0 / math.sqrt(frames_all)
     left_rows = with_quadrature(owned)

time: 548 us -> 523 us (0.954)
  local copies, waits for them, and re-layouts: 107 us -> 79.9 us
    another operation x1 -> x0, local copies, waits for them, and re-layouts: 28.6 us -> none  [channelize(): jnp.stack([spec_real, spec_imag], axis=3)]
where the time goes in v1:
time: 523 us; the launch traced here: 514 us
  matrix products  139 us (27%)
  blocking collectives  137 us (26%)
  waiting for transfers between devices  86.5 us (17%)
  local copies, waits for them, and re-layouts  79.9 us (15%)
  other arithmetic  53.8 us (10%)
  between operations  14.1 us (3%)
    all_to_all x1, blocking collectives, per_device(): lax.all_to_all(jnp.stack(jnp.split(spectra, lax.psum(1, axis_name='ta'),...  137 us
    all_gather x1, waiting for transfers between devices, per_device(): lax.all_gather(owned, 'aa', axis=3, tiled=True)  77.2 us
    concatenate x1, local copies, waits for them, and re-layouts, per_device(): jnp.concatenate([result[:, :signal_count], result[:, signal_count:]], axi...  33.4 us
    concatenate x1, other arithmetic, per_device(): jnp.concatenate([history, voltages], axis=1)  24.4 us
    dot_general x1, matrix products, channelize(): jnp.einsum('sfan,ak->sfkn', blocks, cosine_one, precision=highest)  24 us
    dot_general x1, matrix products, channelize(): jnp.einsum('sfkn,nm->mkfs', twist_imag, sine_two, precision=highest)  22.9 us
    dot_general x1, matrix products, channelize(): jnp.einsum('sfkn,nm->mkfs', twist_imag, cosine_two, precision=highest)  22.5 us
    dot_general x1, matrix products, channelize(): jnp.einsum('sfkn,nm->mkfs', twist_real, sine_two, precision=highest)  18.4 us
  transfers between devices with their start and end apart: 2, of which 2 were waited for; matrix products, arithmetic and copies ran while one was open for 0% of the time, Pallas kernels for 0%

profile of v1, /device:TPU:0, one launch (start us, length us, event | category | flops | bytes accessed | tf_op | source)
XLA Modules:
  0.0 513.6 jit_solution(2793445585837645934)
XLA Ops:
  6.5 0.0 all-gather.2.cloned.1.call-start
  6.5 8.6 %copy.23 = bf16[128,24576]{0,1:T(8,128)(2,1)} copy(bf16[128,24576]{1,0:T(8,128)(2,1)} %param.2) | data formatting | bytes 12582912 | tf_op args[0]
  15.2 2.8 collective-permute-start
  18.0 0.1 fusion.65
  18.1 0.0 copy-done.1
  18.1 0.1 fusion.105
  18.2 9.3 %collective-permute-done = bf16[128,24576]{0,1:T(8,128)(2,1)S(1)} collective-permute-done((bf16[128,24576]{0,1:T(8,128)(2,1)}, bf16[128,24576]{0,1:T(8,128)(2,1)S(1)}, u32[]{:S(2)}, u32[]{:S(2)}) %collective-permute-start) | collective-permute-done | bytes 6291488 | tf_op jit(solution)/shard_map/ppermute | solution.py:16
  27.5 24.4 %pad_maximum_fusion.1 = bf16[128,49152]{0,1:T(8,128)(2,1)S(1)} fusion(bf16[128,24576]{0,1:T(8,128)(2,1)} %copy.23, bf16[128,24576]{0,1:T(8,128)(2,1)S(1)} %collective-permute-done), kind=kLoop, calls=%fused_computation.2 | loop fusion | flops 25165824 | bytes 25165824 | tf_op jit(solution)/shard_map/concatenate | solution.py:77
  52.0 8.4 %multiply_add_fusion = f32[128,3,8192]{0,2,1:T(8,128)} fusion(bf16[128,6,8192]{0,2,1:T(8,128)(2,1)S(1)} %bitcast.116, f32[8192]{0:T(1024)S(1)} %bitcast.124, f32[8192]{0:T(1024)S(1)} %bitcast.125, f32[8192]{0:T(1024)S(1)} %bitcast.123, f32[8192]{0:T(1024)S(1)} %bitcast.122), kind=kLoop, calls=%fused_computation.5 | loop fusion | flops 34603008 | bytes 37879808 | tf_op jit(solution)/shard_map/add | solution.py:67
  60.4 12.8 %copy.25 = f32[128,3,64,128]{3,2,1,0:T(8,128)} copy(f32[128,3,64,128]{0,3,2,1:T(8,128)} %bitcast.119) | data formatting | bytes 25165824 | tf_op jit(solution)/shard_map/reshape | solution.py:42
  73.2 16.9 %fusion.46 = f32[64,128,3,128]{3,0,2,1:T(8,128)} fusion(f32[128,3,64,128]{3,2,1,0:T(8,128)} %copy.25), kind=kOutput, calls=%fused_computation.99 | convolution fusion | flops 2415976448 | bytes 25165824 | tf_op jit(solution)/shard_map/sfan,ak->sfkn/dot_general | solution.py:45
  90.1 24.0 %add_bitcast_fusion = (f32[128,3,64,128]{3,2,1,0:T(8,128)}, f32[128,3,64,128]{3,2,1,0:T(8,128)}) fusion(f32[64,128,3,128]{3,0,2,1:T(8,128)} %fusion.46, f32[64,128]{1,0:T(8,128)S(1)} %get-tuple-element.15, f32[64,128]{1,0:T(8,128)S(1)} %get-tuple-element.16, f32[128,3,64,128]{3,2,1,0:T(8,128)} %copy.25), kind=kOutput, calls=%fused_computation.4 | convolution fusion | flops 2437996544 | bytes 50397184 | tf_op jit(solution)/shard_map/sfan,ak->sfkn/dot_general | solution.py:44
  114.1 22.5 %fusion = f32[32,128,3,64]{1,0,3,2:T(8,128)S(1)} fusion(f32[128,3,64,128]{3,2,1,0:T(8,128)} %get-tuple-element.8, s32[32]{0:T(128)S(1)} %iota_add_fusion), kind=kOutput, calls=%fused_computation.6 | convolution fusion | flops 1208016896 | bytes 15728768 | tf_op jit(solution)/shard_map/sfkn,nm->mkfs/dot_general | solution.py:58
  136.7 0.0 slice-start.2
  136.7 22.9 %fusion.2 = f32[32,128,3,64]{1,0,3,2:T(8,128)S(1)} fusion(f32[128,3,64,128]{3,2,1,0:T(8,128)} %get-tuple-element.8, s32[32]{0:T(128)S(1)} %iota_add_fusion), kind=kOutput, calls=%fused_computation.8 | convolution fusion | flops 1208016896 | bytes 15728768 | tf_op jit(solution)/shard_map/sfkn,nm->mkfs/dot_general | solution.py:55
  159.5 0.0 slice-done
  159.5 0.0 slice-done.1
  159.6 18.3 %fusion.17 = bf16[32,64,3,128]{3,0,1,2:T(8,128)(2,1)S(1)} fusion(f32[32,128,3,64]{1,0,3,2:T(8,128)S(1)} %fusion.2, f32[128,3,64,128]{3,2,1,0:T(8,128)S(1)} %bitcast.118, s32[32]{0:T(128)S(1)} %iota_add_fusion), kind=kOutput, calls=%fused_computation.52 | convolution fusion | flops 1210376192 | bytes 17301632 | tf_op jit(solution)/shard_map/sfkn,nm->mkfs/dot_general | solution.py:54
  177.9 18.4 %fusion.20 = bf16[32,64,3,128]{3,0,1,2:T(8,128)(2,1)S(1)} fusion(f32[32,128,3,64]{1,0,3,2:T(8,128)S(1)} %fusion, f32[128,3,64,128]{3,2,1,0:T(8,128)S(1)} %bitcast.118, s32[32]{0:T(128)S(1)} %iota_add_fusion), kind=kOutput, calls=%fused_computation.53 | convolution fusion | flops 1210376192 | bytes 17301632 | tf_op jit(solution)/shard_map/sfkn,nm->mkfs/dot_general | solution.py:59
  196.2 0.6 copy.32
  196.8 0.6 copy.29
  198.0 137.2 %all_to_all.5 = bf16[16,128,3,2,128]{4,1,2,3,0:T(8,128)(2,1)S(1)} all-to-all(bf16[16,128,3,2,128]{4,1,2,3,0:T(8,128)(2,1)S(1)} %fusion.39), channel_id=1, replica_groups=mesh['ta'=16,'aa'=2] {'ta'}, dimensions={0} | all-to-all | bytes 6291456 | tf_op jit(solution)/shard_map/all_to_all | solution.py:83
  335.2 0.4 copy.33
  335.6 3.7 copy.36
  339.3 0.0 all-gather.2.cloned.1.call-update
  339.3 1.9 copy-done
  341.2 2.0 fusion.104
  343.2 77.2 %all-gather.2.cloned.1.call-done = bf16[128,48,2,256]{3,1,2,0:T(8,128)(2,1)} async-done(((bf16[128,48,2,128]{3,1,2,0:T(8,128)(2,1)}), bf16[128,48,2,256]{3,1,2,0:T(8,128)(2,1)}) %all-gather.2.cloned.1.call-update) | async-done | bytes 6291472 | tf_op jit(solution)/shard_map/all_gather | solution.py:94
  420.4 16.4 %bitcast_multiply_fusion = f32[128,256,256]{1,2,0:T(8,128)} fusion(bf16[128,48,2,256]{3,1,2,0:T(8,128)(2,1)} %all-gather.2.cloned.1.call-done, bf16[128,48,1,128]{3,1,2,0:T(8,128)(2,1)} %get-tuple-element.10, bf16[128,48,1,128]{3,1,2,0:T(8,128)(2,1)} %get-tuple-element.9, bf16[128,48,2,128]{3,1,2,0:T(8,128)(2,1)S(1)} %copy-done), kind=kOutput, calls=%fused_computation.1 | convolution fusion | flops 1637875712 | bytes 46137344 | tf_op jit(solution)/shard_map/cfpi,cfpj->cij/dot_general | solution.py:33
  436.8 17.7 %fusion.103 = (f32[128,128,256]{1,2,0:T(8,128)S(1)}, f32[128,128,256]{1,2,0:T(8,128)}) fusion(f32[128,256,256]{1,2,0:T(8,128)} %bitcast_multiply_fusion), kind=kLoop, calls=%fused_computation.154 | loop fusion | bytes 67108864 | tf_op jit(solution)/shard_map/slice | solution.py:95
  454.6 18.3 %pad_maximum_fusion = f32[128,128,512]{1,2,0:T(8,128)} fusion(f32[128,128,256]{1,2,0:T(8,128)} %get-tuple-element.6, f32[128,128,256]{1,2,0:T(8,128)S(1)} %get-tuple-element.5), kind=kLoop, calls=%fused_computation | loop fusion | flops 8388608 | bytes 67108864 | tf_op jit(solution)/shard_map/concatenate | solution.py:95
  472.9 33.4 %copy.38 = f32[128,128,512]{2,1,0:T(8,128)} copy(f32[128,128,512]{1,2,0:T(8,128)} %pad_maximum_fusion) | data formatting | bytes 67108864 | tf_op jit(solution)/shard_map/concatenate | solution.py:95
  (23 shorter events, 0.4 us)
Async XLA Ops:
  6.5 11.6 %copy-start.1 = (f32[4,8192]{1,0:T(4,128)S(1)}, f32[4,8192]{1,0:T(4,128)}, u32[]{:S(2)}) copy-start(f32[4,8192]{1,0:T(4,128)} %param.3) | copy-start | bytes 393220
  6.5 413.9 %all-gather.2.cloned.1.call-start = ((), (), s32[]{:S(2)}) async-start(), calls=%async_computation.1 | async-start | bytes 9437184 | tf_op jit(solution)/shard_map/all_gather | solution.py:94
  15.2 12.4 %collective-permute-start = (bf16[128,24576]{0,1:T(8,128)(2,1)}, bf16[128,24576]{0,1:T(8,128)(2,1)S(1)}, u32[]{:S(2)}, u32[]{:S(2)}) collective-permute-start(bf16[128,24576]{0,1:T(8,128)(2,1)} %copy.23), channel_id=1, source_target_pairs={{0,2},{2,4},{4,6},{6,8},{8,10},{10,12},{12,14},{14,16},{16,18},{18... | collective-permute-start | bytes 18874376 | tf_op jit(solution)/shard_map/ppermute | solution.py:16
  114.1 45.4 %slice-start = ((s8[12582912]{0:T(1024)(128)(4,1)}), s8[4194304]{0:T(1024)(128)(4,1)S(1)}, s32[]{:S(2)}) async-start(s8[12582912]{0:T(1024)(128)(4,1)} %bitcast.117), calls=%async_computation.2 | async-start | bytes 8388608
  114.1 45.4 %slice-start.1 = ((s8[12582912]{0:T(1024)(128)(4,1)}), s8[4194304]{0:T(1024)(128)(4,1)S(1)}, s32[]{:S(2)}) async-start(s8[12582912]{0:T(1024)(128)(4,1)} %bitcast.117), calls=%async_computation.3 | async-start | bytes 8388608
  136.7 22.9 %slice-start.2 = ((s8[12582912]{0:T(1024)(128)(4,1)}), s8[4194304]{0:T(1024)(128)(4,1)S(1)}, s32[]{:S(2)}) async-start(s8[12582912]{0:T(1024)(128)(4,1)} %bitcast.117), calls=%async_computation.4 | async-start | bytes 8388608
  339.3 1.9 copy-start
Sparse Core Ops, SparseCore 0:
  339.5 80.8 all-gather.1
